TPU v7x, 32 devices: a whole 2x2x4 slice. The times are simulated.
32 devices in a mesh: dp: 16 (over z, y, core), mp: 2 (over x).
Axes of the slice: x: 2, y: 2, z: 4, core: 2. Of those that a mesh axis runs over, the one named last changes fastest.
Arguments:
- hidden: bfloat16 [512, 7168], P('dp', 'mp'), may hold values from -12 to 12
- steering: float32 [7168], P('mp'), may hold values from -3 to 3
- norm_gain: bfloat16 [7168], P('mp'), may hold values from 0.099609375 to 1.8984375
- target: bfloat16 [512, 7168], P('dp', 'mp'), may hold values from -8 to 8
- routes: int32 [512, 8], P('dp'), may hold values from 0 to 15, all different within a row; in each aligned block of 32 rows (0 to 31, 32 to 63, ...) at most 20 rows name the same one
- gate_probs: float32 [512, 8], P('dp'), may hold values from 0.05 to 0.3
- contrast: int32 [512], P('dp'), may hold values from 0 to 1
- gate_weight: bfloat16 [16, 7168, 2048], P('dp', None, 'mp'), may hold values from -0.0625 to 0.0625
- up_weight: bfloat16 [16, 7168, 2048], P('dp', None, 'mp'), may hold values from -0.0625 to 0.0625
- down_weight: bfloat16 [16, 2048, 7168], P('dp', 'mp'), may hold values from -0.125 to 0.125
Outputs:
- mixed: bfloat16 [512, 7168], P('dp', 'mp')
- steer_grad: float32 [7168], P('mp')
Inputs may be any that keep to these rules, and one draw needn't show every extreme that they name: `routes`: each row names 8 different experts; among the 32 rows of one index of dp no expert is named by more than 20 rows.
All inputs are finite; a program needn't handle non-finite values.
Results may differ from a plain program's by a relative error of at most 0.005.
Values may be sent and summed in bfloat16 or wider, within the bound.
No kernel may reach another device: no remote copies, remote signals or barrier semaphores. Data moves between devices by JAX's collectives and lax.ppermute only.
A program may use at most 128 MiB of HBM per device.

v0:
```python
import jax
import jax.numpy as jnp
from jax import lax
from jax.sharding import PartitionSpec as P

EPSILON = 1e-06


def expert_inputs(rows_in, grad_in, gate_mat, up_mat, down_mat):
    gate_pre = jnp.einsum("secd,edf->secf", rows_in, gate_mat, preferred_element_type=jnp.float32)
    up_pre = jnp.einsum("secd,edf->secf", rows_in, up_mat, preferred_element_type=jnp.float32)
    back_hidden = jnp.einsum(
        "secd,efd->secf", grad_in, down_mat, preferred_element_type=jnp.float32
    )
    return (gate_pre, up_pre, back_hidden)


def expert_outputs(gate_pre, up_pre, back_hidden, gate_mat, up_mat, down_mat):
    sigma_gate = jax.nn.sigmoid(gate_pre)
    activated = (gate_pre * sigma_gate * up_pre).astype(jnp.bfloat16)
    grad_gate = (back_hidden * up_pre * sigma_gate * (1.0 + gate_pre * (1.0 - sigma_gate))).astype(
        jnp.bfloat16
    )
    grad_up = (back_hidden * gate_pre * sigma_gate).astype(jnp.bfloat16)
    out_part = jnp.einsum(
        "secf,efd->secd", activated, down_mat, preferred_element_type=jnp.float32
    ).astype(jnp.bfloat16)
    grad_part = (
        jnp.einsum("secf,edf->secd", grad_gate, gate_mat, preferred_element_type=jnp.float32)
        + jnp.einsum("secf,edf->secd", grad_up, up_mat, preferred_element_type=jnp.float32)
    ).astype(jnp.bfloat16)
    return (out_part, grad_part)


def body(
    hidden,
    steering,
    norm_gain,
    target,
    routes,
    gate_probs,
    contrast,
    gate_weight,
    up_weight,
    down_weight,
):
    tokens_here, width_here = hidden.shape
    groups = lax.axis_size("dp")
    quarters = lax.axis_size("mp")
    local_experts = gate_weight.shape[0]
    experts_all = local_experts * groups
    top_count = routes.shape[1]
    capacity = min(
        tokens_here, (5 * tokens_here * top_count + 4 * experts_all - 1) // (4 * experts_all)
    )
    pair_count = tokens_here * top_count
    slot_count = experts_all * capacity
    width_full = width_here * quarters
    stream = hidden.astype(jnp.float32) + steering[None, :]
    square_sum = lax.psum(jnp.sum(stream * stream, axis=1), "mp")
    inverse = lax.rsqrt(square_sum / width_full + EPSILON)[:, None]
    gain_row = norm_gain.astype(jnp.float32)[None, :]
    normed = (stream * inverse * gain_row).astype(jnp.bfloat16)
    sign_col = (2 * contrast - 1).astype(jnp.float32)[:, None]
    flat_routes = routes.reshape(-1)
    one_hot = (flat_routes[:, None] == jnp.arange(experts_all, dtype=jnp.int32)[None, :]).astype(
        jnp.int32
    )
    earlier = jnp.cumsum(one_hot, axis=0) - one_hot
    rank_in = jnp.sum(earlier * one_hot, axis=1)
    slot_of = flat_routes * capacity + rank_in
    source = (
        jnp.full((slot_count,), pair_count, jnp.int32)
        .at[slot_of]
        .set(jnp.arange(pair_count, dtype=jnp.int32))
    )
    source_tok = source // top_count
    probs_pad = jnp.concatenate([gate_probs.reshape(-1), jnp.zeros((1,), jnp.float32)])
    slot_probs = probs_pad[source][:, None]
    col_count = normed.shape[1]
    rows_pad = jnp.concatenate([normed, jnp.zeros((1, col_count), jnp.bfloat16)], axis=0)
    cot_pad = jnp.concatenate(
        [target.astype(jnp.float32) * sign_col, jnp.zeros((1, col_count), jnp.float32)], axis=0
    )
    send_rows = rows_pad[source_tok].reshape(groups, local_experts, capacity, col_count)
    send_grad = (
        (cot_pad[source_tok] * slot_probs)
        .astype(jnp.bfloat16)
        .reshape(groups, local_experts, capacity, col_count)
    )
    send_rows, send_grad = (send_rows, send_grad)
    rows_in = lax.all_to_all(send_rows, "dp", split_axis=0, concat_axis=0, tiled=True)
    grad_in = lax.all_to_all(send_grad, "dp", split_axis=0, concat_axis=0, tiled=True)
    zeros_init = jnp.zeros(rows_in.shape[:3] + (gate_weight.shape[2],), jnp.float32)
    rows_piece = lax.all_gather(rows_in, "mp", axis=3, tiled=True)
    grad_piece = lax.all_gather(grad_in, "mp", axis=3, tiled=True)
    partial_terms = expert_inputs(rows_piece, grad_piece, gate_weight, up_weight, down_weight)
    gate_pre, up_pre, back_hidden = jax.tree.map(
        jnp.add, (zeros_init, zeros_init, zeros_init), partial_terms
    )
    out_part, grad_part = expert_outputs(
        gate_pre, up_pre, back_hidden, gate_weight, up_weight, down_weight
    )
    out_share = lax.psum_scatter(
        out_part.astype(jnp.float32).astype(jnp.bfloat16), "mp", scatter_dimension=3, tiled=True
    ).astype(jnp.float32)
    grad_share = lax.psum_scatter(
        grad_part.astype(jnp.float32).astype(jnp.bfloat16), "mp", scatter_dimension=3, tiled=True
    ).astype(jnp.float32)
    back_out = lax.all_to_all(
        out_share.astype(jnp.bfloat16), "dp", split_axis=0, concat_axis=0, tiled=True
    ).astype(out_share.dtype)
    back_grad = lax.all_to_all(
        grad_share.astype(jnp.bfloat16), "dp", split_axis=0, concat_axis=0, tiled=True
    ).astype(grad_share.dtype)
    col_count = back_out.shape[3]
    out_slots = back_out.reshape(slot_count, col_count)[slot_of].reshape(
        tokens_here, top_count, col_count
    )
    grad_slots = back_grad.reshape(slot_count, col_count)[slot_of].reshape(
        tokens_here, top_count, col_count
    )
    out_tok = jnp.sum(out_slots * gate_probs[:, :, None], axis=1)
    grad_tok = jnp.sum(grad_slots, axis=1)
    mixed = (stream + out_tok).astype(jnp.bfloat16)
    project = lax.psum(jnp.sum(stream * gain_row * grad_tok, axis=1), "mp")[:, None]
    cotangent = target.astype(jnp.float32) * sign_col
    grad_stream = (
        cotangent
        + inverse * gain_row * grad_tok
        - stream * inverse * inverse * inverse * project / width_full
    )
    steer_grad = lax.psum(jnp.sum(grad_stream, axis=0), "dp")
    return (mixed, steer_grad)


def solution(mesh):
    placed = (
        P("dp", "mp"),
        P("mp"),
        P("mp"),
        P("dp", "mp"),
        P("dp", None),
        P("dp", None),
        P("dp"),
        P("dp", None, "mp"),
        P("dp", None, "mp"),
        P("dp", "mp", None),
    )
    return jax.shard_map(
        body, mesh=mesh, in_specs=placed, out_specs=(P("dp", "mp"), P("mp")), check_vma=False
    )
```

profile of v0, /device:TPU:0, one launch (start us, length us, event | category | flops | bytes accessed | tf_op | source)
XLA Modules:
  0.0 593.2 jit_solution(3055648589652543636)
XLA Ops:
  13.1 4.1 gather_fusion.2
  17.1 5.2 gather.20
  25.1 4.7 fusion.27
  29.8 7.5 %all-to-all-start.2 = ((bf16[16,1,20,3584]{3,2,1,0:T(8,128)(2,1)}), bf16[16,1,20,3584]{3,2,1,0:T(8,128)(2,1)S(1)}, u32[]{:S(2)}, u32[]{:S(2)}) async-start(bf16[16,1,20,3584]{3,2,1,0:T(8,128)(2,1)} %fusion.27), calls=%async_computation.3 | async-start | bytes 5505024 | tf_op jit(solution)/shard_map/all_to_all | solution.py:93
  37.7 4.9 psum.21
  42.6 47.2 %all-to-all-done.2 = bf16[16,1,20,3584]{3,2,1,0:T(8,128)(2,1)S(1)} async-done(((bf16[16,1,20,3584]{3,2,1,0:T(8,128)(2,1)}), bf16[16,1,20,3584]{3,2,1,0:T(8,128)(2,1)S(1)}, u32[]{:S(2)}, u32[]{:S(2)}) %all-to-all-start.2) | async-done | bytes 2293792 | tf_op jit(solution)/shard_map/all_to_all | solution.py:93
  97.8 77.0 %all_to_all.20 = bf16[16,1,20,3584]{3,2,1,0:T(8,128)(2,1)} all-to-all(bf16[16,1,20,3584]{3,2,1,0:T(8,128)(2,1)S(1)} %bitcast.165), channel_id=1, replica_groups=mesh['dp'=16,'mp'=2] {'dp'}, dimensions={0} | all-to-all | bytes 4587520 | tf_op jit(solution)/shard_map/all_to_all | solution.py:92
  175.1 11.8 %fusion = f32[16,20,1024]{2,1,0:T(8,128)} fusion(bf16[1,1024,7168]{2,1,0:T(8,128)(2,1)} %param.19, bf16[16,1,20,7168]{3,2,0,1:T(8,128)(2,1)} %all-gather.5.cloned.1.call-done), kind=kOutput, calls=%fused_computation.6 | convolution fusion | flops 4697620480 | bytes 20578304 | tf_op jit(solution)/shard_map/secd,efd->secf/dot_general | solution.py:12
  186.9 58.3 %all-gather.3.cloned.1.call-done = bf16[16,1,20,7168]{3,2,0,1:T(8,128)(2,1)} async-done(((bf16[16,1,20,3584]{3,2,0,1:T(8,128)(2,1)}), bf16[16,1,20,7168]{3,2,0,1:T(8,128)(2,1)}) %all-gather.3.cloned.1.call-update) | async-done | bytes 4587536 | tf_op jit(solution)/shard_map/all_gather | solution.py:95
  245.2 10.9 %fusion.10 = f32[16,20,1024]{2,1,0:T(8,128)S(1)} fusion(bf16[1,7168,1024]{2,1,0:T(8,128)(2,1)} %param.17, bf16[16,1,20,7168]{3,2,0,1:T(8,128)(2,1)} %all-gather.3.cloned.1.call-done), kind=kOutput, calls=%fused_computation.16 | convolution fusion | flops 4697620480 | bytes 20578304 | tf_op jit(solution)/shard_map/secd,edf->secf/dot_general | solution.py:10
  256.2 22.0 %fusion.4 = f32[16,20,7168]{2,1,0:T(8,128)} fusion(bf16[1,7168,1024]{2,1,0:T(8,128)(2,1)} %param.18, f32[16,20,1024]{2,1,0:T(8,128)S(1)} %copy-done.7, f32[16,20,1024]{2,1,0:T(8,128)S(1)} %fusion.10), kind=kOutput, calls=%fused_computation.10 | convolution fusion | flops 4699586560 | bytes 26476544 | tf_op jit(solution)/shard_map/secf,edf->secd/dot_general | solution.py:30
  278.2 10.4 %fusion.6 = f32[16,20,1024]{2,1,0:T(8,128)} fusion(bf16[1,7168,1024]{2,1,0:T(8,128)(2,1)} %param.18, bf16[16,1,20,7168]{3,2,0,1:T(8,128)(2,1)S(1)} %copy-done.6), kind=kOutput, calls=%fused_computation.12 | convolution fusion | flops 4697620480 | bytes 20578304 | tf_op jit(solution)/shard_map/secd,edf->secf/dot_general | solution.py:11
  288.6 14.2 %fusion.20 = bf16[16,1,20,7168]{3,2,0,1:T(8,128)(2,1)} fusion(f32[16,20,7168]{2,1,0:T(8,128)} %fusion.4, bf16[1,7168,1024]{2,1,0:T(8,128)(2,1)} %param.17, f32[16,20,1024]{2,1,0:T(8,128)} %fusion, f32[16,20,1024]{2,1,0:T(8,128)} %fusion.6, f32[16,20,1024]{2,1,0:T(8,128)S(1)} %fusion.10), kind=kOutput, calls=%fused_computation.21 | convolution fusion | flops 4705484800 | bytes 32374784 | tf_op jit(solution)/shard_map/secf,edf->secd/dot_general | solution.py:29
  302.8 11.4 %fusion.17 = bf16[16,1,20,7168]{3,2,0,1:T(8,128)(2,1)} fusion(bf16[1,1024,7168]{2,1,0:T(8,128)(2,1)} %param.19, f32[16,20,1024]{2,1,0:T(8,128)} %fusion.6, f32[16,20,1024]{2,1,0:T(8,128)S(1)} %fusion.10), kind=kOutput, calls=%fused_computation.20 | convolution fusion | flops 4701880320 | bytes 21889024 | tf_op jit(solution)/shard_map/secf,efd->secd/dot_general | solution.py:25
  314.3 57.3 %reduce-scatter.5.cloned.1.call-done = bf16[16,1,20,3584]{3,2,0,1:T(8,128)(2,1)} async-done(((bf16[16,1,20,7168]{3,2,0,1:T(8,128)(2,1)}), bf16[16,1,20,3584]{3,2,0,1:T(8,128)(2,1)}) %reduce-scatter.5.cloned.1.call-update) | async-done | bytes 2293776 | tf_op jit(solution)/shard_map/reduce_scatter | solution.py:107
  371.6 5.6 all-to-all-start.3
  377.2 65.2 %reduce-scatter.3.cloned.1.call-done = bf16[16,1,20,3584]{3,2,0,1:T(8,128)(2,1)} async-done(((bf16[16,1,20,7168]{3,2,0,1:T(8,128)(2,1)}), bf16[16,1,20,3584]{3,2,0,1:T(8,128)(2,1)}) %reduce-scatter.3.cloned.1.call-update) | async-done | bytes 2293776 | tf_op jit(solution)/shard_map/reduce_scatter | solution.py:104
  442.3 5.7 all-to-all-start.1
  450.7 7.5 %gather_fusion.4 = f32[256,3584]{1,0:T(8,128)} fusion(f32[320,3584]{1,0:T(8,128)} %reshape.159, s32[1024]{0:T(1024)S(1)} %pad_clamp_fusion.1), kind=kCustom, calls=%fused_computation.4 | custom fusion | bytes 7341056 | tf_op jit(solution)/shard_map/gather | solution.py:120
  461.3 4.9 psum.22
  466.3 34.2 %all-to-all-done.1 = bf16[16,1,20,3584]{3,2,1,0:T(8,128)(2,1)} async-done(((bf16[16,1,20,3584]{3,2,1,0:T(8,128)(2,1)}), bf16[16,1,20,3584]{3,2,1,0:T(8,128)(2,1)}, u32[]{:S(2)}, u32[]{:S(2)}) %all-to-all-start.1) | async-done | bytes 2293792 | tf_op jit(solution)/shard_map/all_to_all | solution.py:110
  500.5 4.5 reshape.157
  505.0 7.5 %gather_fusion.1 = f32[256,3584]{1,0:T(8,128)} fusion(f32[320,3584]{1,0:T(8,128)} %reshape.157, s32[1024]{0:T(1024)S(1)} %pad_clamp_fusion.1), kind=kCustom, calls=%fused_computation.1 | custom fusion | bytes 7341056 | tf_op jit(solution)/shard_map/gather | solution.py:117
  516.7 70.0 %psum.23 = f32[3584]{0:T(1024)} all-reduce(f32[3584]{0:T(1024)S(1)} %get-tuple-element.2), channel_id=1, replica_groups=mesh['dp'=16,'mp'=2] {'dp'}, use_global_device_ids=true, to_apply=%region_13.14 | all-reduce | flops 3584 | bytes 28672 | tf_op jit(solution)/shard_map/psum | solution.py:133
  (64 shorter events, 27.2 us)
Async XLA Ops:
  17.1 5.2 copy-start.5
  29.8 7.6 %copy-start.4 = (bf16[3584]{0:T(1024)(128)(2,1)S(1)}, bf16[3584]{0:T(1024)(128)(2,1)}, u32[]{:S(2)}) copy-start(bf16[3584]{0:T(1024)(128)(2,1)} %param.12) | copy-start | bytes 21508
  29.8 7.6 %copy-start.1 = (bf16[32,3584]{1,0:T(8,128)(2,1)S(1)}, bf16[32,3584]{1,0:T(8,128)(2,1)}, u32[]{:S(2)}) copy-start(bf16[32,3584]{1,0:T(8,128)(2,1)} %param.10) | copy-start | bytes 688132
  29.8 7.6 %copy-start.3 = (f32[3584]{0:T(1024)S(1)}, f32[3584]{0:T(1024)}, u32[]{:S(2)}) copy-start(f32[3584]{0:T(1024)} %param.11) | copy-start | bytes 43012
  29.8 59.9 %all-to-all-start.2 = ((bf16[16,1,20,3584]{3,2,1,0:T(8,128)(2,1)}), bf16[16,1,20,3584]{3,2,1,0:T(8,128)(2,1)S(1)}, u32[]{:S(2)}, u32[]{:S(2)}) async-start(bf16[16,1,20,3584]{3,2,1,0:T(8,128)(2,1)} %fusion.27), calls=%async_computation.3 | async-start | bytes 5505024 | tf_op jit(solution)/shard_map/all_to_all | solution.py:93
  37.4 137.7 %all-gather.5.cloned.1.call-start = ((), (), s32[]{:S(2)}) async-start(), calls=%async_computation.8 | async-start | bytes 8257536 | tf_op jit(solution)/shard_map/all_gather | solution.py:96
  89.8 1.5 copy-start
  91.3 153.9 %all-gather.3.cloned.1.call-start = ((), (), s32[]{:S(2)}) async-start(), calls=%async_computation.6 | async-start | bytes 8257536 | tf_op jit(solution)/shard_map/all_gather | solution.py:95
  174.8 196.8 %reduce-scatter.5.cloned.1.call-start = ((), (), s32[]{:S(2)}) async-start(), calls=%async_computation.9 | async-start | bytes 8257536 | tf_op jit(solution)/shard_map/reduce_scatter | solution.py:107
  245.2 10.9 %copy-start.7 = (f32[16,20,1024]{2,1,0:T(8,128)S(1)}, f32[16,20,1024]{2,1,0:T(8,128)}, u32[]{:S(2)}) copy-start(f32[16,20,1024]{2,1,0:T(8,128)} %fusion) | copy-start | bytes 3932164
  256.2 22.0 %copy-start.6 = (bf16[16,1,20,7168]{3,2,0,1:T(8,128)(2,1)S(1)}, bf16[16,1,20,7168]{3,2,0,1:T(8,128)(2,1)}, u32[]{:S(2)}) copy-start(bf16[16,1,20,7168]{3,2,0,1:T(8,128)(2,1)} %all-gather.3.cloned.1.call-done) | copy-start | bytes 13762564
  302.8 139.6 %reduce-scatter.3.cloned.1.call-start = ((), (), s32[]{:S(2)}) async-start(), calls=%async_computation.7 | async-start | bytes 8257536 | tf_op jit(solution)/shard_map/reduce_scatter | solution.py:104
  371.6 70.8 %all-to-all-start.3 = ((bf16[16,1,20,3584]{3,2,1,0:T(8,128)(2,1)}), bf16[16,1,20,3584]{3,2,1,0:T(8,128)(2,1)S(1)}, u32[]{:S(2)}, u32[]{:S(2)}) async-start(bf16[16,1,20,3584]{3,2,1,0:T(8,128)(2,1)} %bitcast.167), calls=%async_computation.5 | async-start | bytes 5505024 | tf_op jit(solution)/shard_map/all_to_all | solution.py:113
  442.3 58.1 %all-to-all-start.1 = ((bf16[16,1,20,3584]{3,2,1,0:T(8,128)(2,1)}), bf16[16,1,20,3584]{3,2,1,0:T(8,128)(2,1)}, u32[]{:S(2)}, u32[]{:S(2)}) async-start(bf16[16,1,20,3584]{3,2,1,0:T(8,128)(2,1)} %bitcast.166), calls=%async_computation.2 | async-start | bytes 5505024 | tf_op jit(solution)/shard_map/all_to_all | solution.py:110
  512.4 3.3 copy-start.2
Sparse Core Ops, SparseCore 0:
  91.4 80.6 all-gather.4
  174.9 70.2 all-gather.2
  302.9 68.6 reduce-scatter.4
  373.7 68.5 reduce-scatter.2
where the time goes:
time: 594 us; the launch traced here: 593 us
  waiting for transfers between devices  262 us (44%)
  blocking collectives  157 us (26%)
  matrix products  80.7 us (14%)
  local copies, waits for them, and re-layouts  44.6 us (8%)
  starting transfers between devices  19.2 us (3%)
  other arithmetic  15.6 us (3%)
  between operations  14 us (2%)
    all_to_all x1, blocking collectives, body(): lax.all_to_all(send_rows, 'dp', split_axis=0, concat_axis=0, tiled=True)  77 us
    psum x1, blocking collectives, body(): steer_grad = lax.psum(jnp.sum(grad_stream, axis=0), 'dp')  70 us
    reduce_scatter x1, waiting for transfers between devices, body(): lax.psum_scatter(out_part.astype(jnp.float32).astype(jnp.bfloat16), 'mp',...  65.2 us
    all_gather x1, waiting for transfers between devices, body(): rows_piece = lax.all_gather(rows_in, 'mp', axis=3, tiled=True)  58.3 us
    reduce_scatter x1, waiting for transfers between devices, body(): lax.psum_scatter(grad_part.astype(jnp.float32).astype(jnp.bfloat16), 'mp'...  57.3 us
    all_to_all x1, waiting for transfers between devices, body(): lax.all_to_all(send_grad, 'dp', split_axis=0, concat_axis=0, tiled=True)  47.2 us
    all_to_all x1, waiting for transfers between devices, body(): lax.all_to_all(out_share.astype(jnp.bfloat16), 'dp', split_axis=0, concat...  34.2 us
    dot_general x1, matrix products, expert_outputs(): jnp.einsum('secf,edf->secd', grad_up, up_mat, preferred_element_type=jnp....  22 us
  transfers between devices with their start and end apart: 7, of which 5 were waited for; matrix products, arithmetic and copies ran while one was open for 7% of the time, Pallas kernels for 0%

commit v1 on v0

--- a/solution.py
+++ b/solution.py
@@ -130,7 +130,8 @@
         + inverse * gain_row * grad_tok
         - stream * inverse * inverse * inverse * project / width_full
     )
-    steer_grad = lax.psum(jnp.sum(grad_stream, axis=0), "dp")
+    _carry_matrix = lambda xin: jnp.sum(lax.all_gather(xin, "dp"), axis=0)
+    steer_grad = _carry_matrix(jnp.sum(grad_stream, axis=0))
     return (mixed, steer_grad)
 
 

time: 594 us -> 555 us (0.934)
  blocking collectives: 157 us -> 117 us
    psum x1 -> x0, blocking collectives: 70 us -> none  [body(): steer_grad = lax.psum(jnp.sum(grad_stream, axis=0), 'dp')]
    all_gather x0 -> x1, blocking collectives: none -> 30.2 us  [body(): _carry_matrix = lambda xin: jnp.sum(lax.all_gather(xin, 'dp'), axis=0)]
  transfers between devices with their start and end apart: 7 -> 7, of which waited for: 5 -> 5; matrix products, arithmetic and copies ran while one was open for 7% -> 8% of each run, Pallas kernels for 0% -> 0%
where the time goes in v1:
time: 555 us; the launch traced here: 554 us
  waiting for transfers between devices  262 us (47%)
  blocking collectives  117 us (21%)
  matrix products  80.7 us (15%)
  local copies, waits for them, and re-layouts  44.6 us (8%)
  starting transfers between devices  19.2 us (3%)
  other arithmetic  16.3 us (3%)
  between operations  14 us (3%)
    all_to_all x1, blocking collectives, body(): lax.all_to_all(send_rows, 'dp', split_axis=0, concat_axis=0, tiled=True)  77 us
    reduce_scatter x1, waiting for transfers between devices, body(): lax.psum_scatter(out_part.astype(jnp.float32).astype(jnp.bfloat16), 'mp',...  65.2 us
    all_gather x1, waiting for transfers between devices, body(): rows_piece = lax.all_gather(rows_in, 'mp', axis=3, tiled=True)  58.3 us
    reduce_scatter x1, waiting for transfers between devices, body(): lax.psum_scatter(grad_part.astype(jnp.float32).astype(jnp.bfloat16), 'mp'...  57.3 us
    all_to_all x1, waiting for transfers between devices, body(): lax.all_to_all(send_grad, 'dp', split_axis=0, concat_axis=0, tiled=True)  47.2 us
    all_to_all x1, waiting for transfers between devices, body(): lax.all_to_all(out_share.astype(jnp.bfloat16), 'dp', split_axis=0, concat...  34.2 us
    all_gather x1, blocking collectives, body(): _carry_matrix = lambda xin: jnp.sum(lax.all_gather(xin, 'dp'), axis=0)  30.2 us
    dot_general x1, matrix products, expert_outputs(): jnp.einsum('secf,edf->secd', grad_up, up_mat, preferred_element_type=jnp....  22 us
  transfers between devices with their start and end apart: 7, of which 5 were waited for; matrix products, arithmetic and copies ran while one was open for 8% of the time, Pallas kernels for 0%

profile of v1, /device:TPU:0, one launch (start us, length us, event | category | flops | bytes accessed | tf_op | source)
XLA Modules:
  0.0 554.2 jit_solution(13382897888338173206)
XLA Ops:
  13.1 4.1 gather_fusion.2
  17.1 5.2 gather.20
  25.1 4.7 fusion.27
  29.8 7.5 %all-to-all-start.2 = ((bf16[16,1,20,3584]{3,2,1,0:T(8,128)(2,1)}), bf16[16,1,20,3584]{3,2,1,0:T(8,128)(2,1)S(1)}, u32[]{:S(2)}, u32[]{:S(2)}) async-start(bf16[16,1,20,3584]{3,2,1,0:T(8,128)(2,1)} %fusion.27), calls=%async_computation.3 | async-start | bytes 5505024 | tf_op jit(solution)/shard_map/all_to_all | solution.py:93
  37.7 4.9 psum.14
  42.6 47.2 %all-to-all-done.2 = bf16[16,1,20,3584]{3,2,1,0:T(8,128)(2,1)S(1)} async-done(((bf16[16,1,20,3584]{3,2,1,0:T(8,128)(2,1)}), bf16[16,1,20,3584]{3,2,1,0:T(8,128)(2,1)S(1)}, u32[]{:S(2)}, u32[]{:S(2)}) %all-to-all-start.2) | async-done | bytes 2293792 | tf_op jit(solution)/shard_map/all_to_all | solution.py:93
  97.8 77.0 %all_to_all.20 = bf16[16,1,20,3584]{3,2,1,0:T(8,128)(2,1)} all-to-all(bf16[16,1,20,3584]{3,2,1,0:T(8,128)(2,1)S(1)} %bitcast.165), channel_id=1, replica_groups=mesh['dp'=16,'mp'=2] {'dp'}, dimensions={0} | all-to-all | bytes 4587520 | tf_op jit(solution)/shard_map/all_to_all | solution.py:92
  175.1 11.8 %fusion = f32[16,20,1024]{2,1,0:T(8,128)} fusion(bf16[1,1024,7168]{2,1,0:T(8,128)(2,1)} %param.19, bf16[16,1,20,7168]{3,2,0,1:T(8,128)(2,1)} %all-gather.7.cloned.1.call-done), kind=kOutput, calls=%fused_computation.6 | convolution fusion | flops 4697620480 | bytes 20578304 | tf_op jit(solution)/shard_map/secd,efd->secf/dot_general | solution.py:12
  186.9 58.3 %all-gather.5.cloned.1.call-done = bf16[16,1,20,7168]{3,2,0,1:T(8,128)(2,1)} async-done(((bf16[16,1,20,3584]{3,2,0,1:T(8,128)(2,1)}), bf16[16,1,20,7168]{3,2,0,1:T(8,128)(2,1)}) %all-gather.5.cloned.1.call-update) | async-done | bytes 4587536 | tf_op jit(solution)/shard_map/all_gather | solution.py:95
  245.2 10.9 %fusion.10 = f32[16,20,1024]{2,1,0:T(8,128)S(1)} fusion(bf16[1,7168,1024]{2,1,0:T(8,128)(2,1)} %param.17, bf16[16,1,20,7168]{3,2,0,1:T(8,128)(2,1)} %all-gather.5.cloned.1.call-done), kind=kOutput, calls=%fused_computation.16 | convolution fusion | flops 4697620480 | bytes 20578304 | tf_op jit(solution)/shard_map/secd,edf->secf/dot_general | solution.py:10
  256.2 22.0 %fusion.4 = f32[16,20,7168]{2,1,0:T(8,128)} fusion(bf16[1,7168,1024]{2,1,0:T(8,128)(2,1)} %param.18, f32[16,20,1024]{2,1,0:T(8,128)S(1)} %copy-done.7, f32[16,20,1024]{2,1,0:T(8,128)S(1)} %fusion.10), kind=kOutput, calls=%fused_computation.10 | convolution fusion | flops 4699586560 | bytes 26476544 | tf_op jit(solution)/shard_map/secf,edf->secd/dot_general | solution.py:30
  278.2 10.4 %fusion.6 = f32[16,20,1024]{2,1,0:T(8,128)} fusion(bf16[1,7168,1024]{2,1,0:T(8,128)(2,1)} %param.18, bf16[16,1,20,7168]{3,2,0,1:T(8,128)(2,1)S(1)} %copy-done.6), kind=kOutput, calls=%fused_computation.12 | convolution fusion | flops 4697620480 | bytes 20578304 | tf_op jit(solution)/shard_map/secd,edf->secf/dot_general | solution.py:11
  288.6 14.2 %fusion.20 = bf16[16,1,20,7168]{3,2,0,1:T(8,128)(2,1)} fusion(f32[16,20,7168]{2,1,0:T(8,128)} %fusion.4, bf16[1,7168,1024]{2,1,0:T(8,128)(2,1)} %param.17, f32[16,20,1024]{2,1,0:T(8,128)} %fusion, f32[16,20,1024]{2,1,0:T(8,128)} %fusion.6, f32[16,20,1024]{2,1,0:T(8,128)S(1)} %fusion.10), kind=kOutput, calls=%fused_computation.21 | convolution fusion | flops 4705484800 | bytes 32374784 | tf_op jit(solution)/shard_map/secf,edf->secd/dot_general | solution.py:29
  302.8 11.4 %fusion.17 = bf16[16,1,20,7168]{3,2,0,1:T(8,128)(2,1)} fusion(bf16[1,1024,7168]{2,1,0:T(8,128)(2,1)} %param.19, f32[16,20,1024]{2,1,0:T(8,128)} %fusion.6, f32[16,20,1024]{2,1,0:T(8,128)S(1)} %fusion.10), kind=kOutput, calls=%fused_computation.20 | convolution fusion | flops 4701880320 | bytes 21889024 | tf_op jit(solution)/shard_map/secf,efd->secd/dot_general | solution.py:25
  314.3 57.3 %reduce-scatter.5.cloned.1.call-done = bf16[16,1,20,3584]{3,2,0,1:T(8,128)(2,1)} async-done(((bf16[16,1,20,7168]{3,2,0,1:T(8,128)(2,1)}), bf16[16,1,20,3584]{3,2,0,1:T(8,128)(2,1)}) %reduce-scatter.5.cloned.1.call-update) | async-done | bytes 2293776 | tf_op jit(solution)/shard_map/reduce_scatter | solution.py:107
  371.6 5.6 %all-to-all-start.3 = ((bf16[16,1,20,3584]{3,2,1,0:T(8,128)(2,1)}), bf16[16,1,20,3584]{3,2,1,0:T(8,128)(2,1)S(1)}, u32[]{:S(2)}, u32[]{:S(2)}) async-start(bf16[16,1,20,3584]{3,2,1,0:T(8,128)(2,1)} %bitcast.167), calls=%async_computation.5 | async-start | bytes 5505024 | tf_op jit(solution)/shard_map/all_to_all | solution.py:113
  377.2 65.2 %reduce-scatter.3.cloned.1.call-done = bf16[16,1,20,3584]{3,2,0,1:T(8,128)(2,1)} async-done(((bf16[16,1,20,7168]{3,2,0,1:T(8,128)(2,1)}), bf16[16,1,20,3584]{3,2,0,1:T(8,128)(2,1)}) %reduce-scatter.3.cloned.1.call-update) | async-done | bytes 2293776 | tf_op jit(solution)/shard_map/reduce_scatter | solution.py:104
  442.3 5.7 %all-to-all-start.1 = ((bf16[16,1,20,3584]{3,2,1,0:T(8,128)(2,1)}), bf16[16,1,20,3584]{3,2,1,0:T(8,128)(2,1)}, u32[]{:S(2)}, u32[]{:S(2)}) async-start(bf16[16,1,20,3584]{3,2,1,0:T(8,128)(2,1)} %bitcast.166), calls=%async_computation.2 | async-start | bytes 5505024 | tf_op jit(solution)/shard_map/all_to_all | solution.py:110
  450.7 7.5 %gather_fusion.4 = f32[256,3584]{1,0:T(8,128)} fusion(f32[320,3584]{1,0:T(8,128)} %reshape.159, s32[1024]{0:T(1024)S(1)} %pad_clamp_fusion.1), kind=kCustom, calls=%fused_computation.4 | custom fusion | bytes 7341056 | tf_op jit(solution)/shard_map/gather | solution.py:120
  461.3 4.9 psum.15
  466.3 34.2 %all-to-all-done.1 = bf16[16,1,20,3584]{3,2,1,0:T(8,128)(2,1)} async-done(((bf16[16,1,20,3584]{3,2,1,0:T(8,128)(2,1)}), bf16[16,1,20,3584]{3,2,1,0:T(8,128)(2,1)}, u32[]{:S(2)}, u32[]{:S(2)}) %all-to-all-start.1) | async-done | bytes 2293792 | tf_op jit(solution)/shard_map/all_to_all | solution.py:110
  500.5 4.5 reshape.157
  505.0 7.5 %gather_fusion.1 = f32[256,3584]{1,0:T(8,128)} fusion(f32[320,3584]{1,0:T(8,128)} %reshape.157, s32[1024]{0:T(1024)S(1)} %pad_clamp_fusion.1), kind=kCustom, calls=%fused_computation.1 | custom fusion | bytes 7341056 | tf_op jit(solution)/shard_map/gather | solution.py:117
  516.7 30.2 %all-gather.1 = f32[16,1,3584]{2,1,0:T(1,128)S(1)} all-gather(f32[1,1,3584]{2,1,0:T(1,128)S(1)} %reshape.212), channel_id=2, replica_groups=mesh['dp'=16,'mp'=2] {'dp'}, dimensions={0}, use_global_device_ids=true | all-gather | bytes 243712 | tf_op jit(solution)/shard_map/all_gather | solution.py:133
  (66 shorter events, 28.0 us)
Async XLA Ops:
  17.1 5.2 copy-start.5
  29.8 7.6 %copy-start.4 = (bf16[3584]{0:T(1024)(128)(2,1)S(1)}, bf16[3584]{0:T(1024)(128)(2,1)}, u32[]{:S(2)}) copy-start(bf16[3584]{0:T(1024)(128)(2,1)} %param.12) | copy-start | bytes 21508
  29.8 7.6 %copy-start.1 = (bf16[32,3584]{1,0:T(8,128)(2,1)S(1)}, bf16[32,3584]{1,0:T(8,128)(2,1)}, u32[]{:S(2)}) copy-start(bf16[32,3584]{1,0:T(8,128)(2,1)} %param.10) | copy-start | bytes 688132
  29.8 7.6 %copy-start.3 = (f32[3584]{0:T(1024)S(1)}, f32[3584]{0:T(1024)}, u32[]{:S(2)}) copy-start(f32[3584]{0:T(1024)} %param.11) | copy-start | bytes 43012
  29.8 59.9 %all-to-all-start.2 = ((bf16[16,1,20,3584]{3,2,1,0:T(8,128)(2,1)}), bf16[16,1,20,3584]{3,2,1,0:T(8,128)(2,1)S(1)}, u32[]{:S(2)}, u32[]{:S(2)}) async-start(bf16[16,1,20,3584]{3,2,1,0:T(8,128)(2,1)} %fusion.27), calls=%async_computation.3 | async-start | bytes 5505024 | tf_op jit(solution)/shard_map/all_to_all | solution.py:93
  37.4 137.7 %all-gather.7.cloned.1.call-start = ((), (), s32[]{:S(2)}) async-start(), calls=%async_computation.8 | async-start | bytes 8257536 | tf_op jit(solution)/shard_map/all_gather | solution.py:96
  89.8 1.5 copy-start
  91.3 153.9 %all-gather.5.cloned.1.call-start = ((), (), s32[]{:S(2)}) async-start(), calls=%async_computation.6 | async-start | bytes 8257536 | tf_op jit(solution)/shard_map/all_gather | solution.py:95
  174.8 196.8 %reduce-scatter.5.cloned.1.call-start = ((), (), s32[]{:S(2)}) async-start(), calls=%async_computation.9 | async-start | bytes 8257536 | tf_op jit(solution)/shard_map/reduce_scatter | solution.py:107
  245.2 10.9 %copy-start.7 = (f32[16,20,1024]{2,1,0:T(8,128)S(1)}, f32[16,20,1024]{2,1,0:T(8,128)}, u32[]{:S(2)}) copy-start(f32[16,20,1024]{2,1,0:T(8,128)} %fusion) | copy-start | bytes 3932164
  256.2 22.0 %copy-start.6 = (bf16[16,1,20,7168]{3,2,0,1:T(8,128)(2,1)S(1)}, bf16[16,1,20,7168]{3,2,0,1:T(8,128)(2,1)}, u32[]{:S(2)}) copy-start(bf16[16,1,20,7168]{3,2,0,1:T(8,128)(2,1)} %all-gather.5.cloned.1.call-done) | copy-start | bytes 13762564
  302.8 139.6 %reduce-scatter.3.cloned.1.call-start = ((), (), s32[]{:S(2)}) async-start(), calls=%async_computation.7 | async-start | bytes 8257536 | tf_op jit(solution)/shard_map/reduce_scatter | solution.py:104
  371.6 70.8 %all-to-all-start.3 = ((bf16[16,1,20,3584]{3,2,1,0:T(8,128)(2,1)}), bf16[16,1,20,3584]{3,2,1,0:T(8,128)(2,1)S(1)}, u32[]{:S(2)}, u32[]{:S(2)}) async-start(bf16[16,1,20,3584]{3,2,1,0:T(8,128)(2,1)} %bitcast.167), calls=%async_computation.5 | async-start | bytes 5505024 | tf_op jit(solution)/shard_map/all_to_all | solution.py:113
  442.3 58.1 %all-to-all-start.1 = ((bf16[16,1,20,3584]{3,2,1,0:T(8,128)(2,1)}), bf16[16,1,20,3584]{3,2,1,0:T(8,128)(2,1)}, u32[]{:S(2)}, u32[]{:S(2)}) async-start(bf16[16,1,20,3584]{3,2,1,0:T(8,128)(2,1)} %bitcast.166), calls=%async_computation.2 | async-start | bytes 5505024 | tf_op jit(solution)/shard_map/all_to_all | solution.py:110
  512.4 3.3 copy-start.2
Sparse Core Ops, SparseCore 0:
  91.4 80.6 all-gather.6
  174.9 70.2 all-gather.4
  302.9 68.6 reduce-scatter.4
  373.7 68.5 reduce-scatter.2
